TPU v7x, 32 devices: a whole 2x2x4 slice. The times are simulated.
32 devices in a mesh: groups: 2 (over y), rows: 4 (over z), cols: 4 (over x, core).
Axes of the slice: x: 2, y: 2, z: 4, core: 2. Of those that a mesh axis runs over, the one named last changes fastest.
Arguments:
- tile_blocks: float32 [32, 32, 4, 128, 128], P(('groups', 'rows'), 'cols'), parts along dimension 0, may hold values from -1 to 3
- tile_codes: int32 [32, 32, 3], P(('groups', 'rows'), 'cols'), parts along dimension 0, may hold values from 0 to 3, as said below
- shifts: float32 [16], P('groups'), parts along dimension 0, may hold values from 1.2 to 2.8
- shift_order: int32 [16], P('groups'), parts along dimension 0, may hold values from 0 to 7, each once
- earlier: float32 [16, 32, 32, 128], P(None, ('groups', 'rows'), 'cols'), parts along dimension 1, may hold values from -60 to 60
- start_weights: float32 [32], P('groups'), parts along dimension 0, may hold values from -1 to 1
Outputs:
- new_basis: float32 [8, 32, 32, 128], P(None, ('groups', 'rows'), 'cols'), parts along dimension 1
- upper_factor: float32 [16, 8], P('groups'), parts along dimension 0
- projections: float32 [32, 8], P('groups'), parts along dimension 0
There are 2 independent parts, one for each index of `groups`. A program takes and returns all parts, laid end to end along the dimension named above; each array names one. Nothing has to cross between parts.
Inputs may be any that keep to these rules, and one draw needn't show every extreme that they name: `tile_codes`: the three codes of one block are distinct. `shift_order`: each of 0 to 7 appears once.
All inputs are finite; a program needn't handle non-finite values.
Results may differ from a plain program's by a relative error of at most 0.0003.
Values sent between devices are 32-bit elements; how exact they have to be, the bound alone decides.
A program may use at most 64 MiB of HBM per device.

v0:
```python
import functools

import jax
import jax.numpy as jnp
from jax import lax
from jax.experimental import pallas as pl
from jax.experimental.pallas import tpu as pltpu
from jax.sharding import PartitionSpec as P

MESH = pl.DeviceIdType.MESH
ABOVE, BELOW, LEFT, RIGHT = range(4)


def kernel(
    n_rows, n_cols, pitch,
    blocks_hbm, codes_hbm, shifts_hbm, order_hbm, earlier_hbm, weights_hbm,
    basis_ref, upper_ref, proj_ref,
    blocks, earlier, codes_ref, shifts_ref, order_ref, weights_ref,
    fields, chosen, halo_rows, halo_cols, edge_cols, rim_rows, rim_cols,
    code_table, stats, gathered, spread,
    load_sem, small_sem, send_sem, recv_sem, all_send, all_recv,
):
    rows, cols, slots, tile, _ = blocks.shape
    basis = basis_ref.shape[0]
    prev = earlier.shape[0]
    groups_prev = prev // basis
    peers = n_rows * n_cols
    cells = float(peers * rows * cols * tile)
    my_row, my_col = lax.axis_index("rows"), lax.axis_index("cols")
    me = my_row * n_cols + my_col

    def load(r, c):
        return pltpu.make_async_copy(
            blocks_hbm.at[r, c], blocks.at[r, c], load_sem.at[r, c]
        )

    small = [
        pltpu.make_async_copy(src, dst, small_sem.at[i])
        for i, (src, dst) in enumerate(
            [
                (weights_hbm, weights_ref),
                (earlier_hbm, earlier),
                (codes_hbm, codes_ref),
                (shifts_hbm, shifts_ref),
                (order_hbm, order_ref),
            ]
        )
    ]
    for copy in small:
        copy.start()
    for r in range(rows):
        for c in range(cols):
            load(r, c).start()

    barrier = pltpu.get_barrier_semaphore()

    def place(index):
        return {"rows": index // n_cols, "cols": index % n_cols}

    @pl.loop(1, peers)
    def _(d):
        pl.semaphore_signal(
            barrier, inc=1, device_id=place((me + d) % peers), device_id_type=MESH
        )

    for k in range(1, basis + 1):
        fields[k] = jnp.zeros((rows, cols, tile), jnp.float32)
    stats[...] = jnp.zeros_like(stats)
    no_row = jnp.zeros((basis, cols, tile), jnp.float32)
    no_col = jnp.zeros((basis, rows, tile), jnp.float32)
    has = [my_row > 0, my_row < n_rows - 1, my_col > 0, my_col < n_cols - 1]

    @pl.when(my_row == 0)
    def _():
        halo_rows[:, 0] = no_row

    @pl.when(my_row == n_rows - 1)
    def _():
        halo_rows[:, 1] = no_row

    @pl.when(my_col == 0)
    def _():
        halo_cols[:, 0] = no_col

    @pl.when(my_col == n_cols - 1)
    def _():
        halo_cols[:, 1] = no_col

    def hop(k, direction):
        if direction == ABOVE:
            src, dst, where_to = fields.at[k, 0], halo_rows.at[k, 1], {"rows": my_row - 1}
        elif direction == BELOW:
            src, dst, where_to = fields.at[k, rows - 1], halo_rows.at[k, 0], {"rows": my_row + 1}
        elif direction == LEFT:
            src, dst, where_to = edge_cols.at[k, 0], halo_cols.at[k, 1], {"cols": my_col - 1}
        else:
            src, dst, where_to = edge_cols.at[k, 1], halo_cols.at[k, 0], {"cols": my_col + 1}
        return pltpu.make_async_remote_copy(
            src_ref=src,
            dst_ref=dst,
            send_sem=send_sem.at[k, direction],
            recv_sem=recv_sem.at[k, direction ^ 1],
            device_id=where_to,
            device_id_type=MESH,
        )

    def arrival(k, direction):
        if direction in (ABOVE, BELOW):
            dst = halo_rows.at[k, direction]
        else:
            dst = halo_cols.at[k, direction - 2]
        return pltpu.make_async_copy(dst, dst, recv_sem.at[k, direction])

    def send(k, directions):
        for direction in directions:
            @pl.when(has[direction])
            def _(direction=direction):
                hop(k, direction).start()

    def receive(k):
        for direction in range(4):
            @pl.when(has[direction])
            def _(direction=direction):
                arrival(k, direction).wait()

    sublane = lax.broadcasted_iota(jnp.int32, (cols, tile), 0)
    lane = lax.broadcasted_iota(jnp.int32, (basis, tile), 1)
    diagonal = lax.broadcasted_iota(jnp.int32, (cols, cols), 0) == lax.broadcasted_iota(
        jnp.int32, (cols, cols), 1
    )

    def code_columns():
        codes = codes_ref[...].astype(jnp.float32)
        masks = []
        for s in range(slots - 1):
            masks.append([])
            for r in range(rows):
                line = jnp.broadcast_to(codes[s, r : r + 1], (cols, cols))
                column = jnp.sum(jnp.where(diagonal, line, 0.0), axis=1, keepdims=True)
                masks[s].append(jnp.broadcast_to(column, (cols, tile)))
        return masks

    def choose(k):
        none = jnp.zeros((cols, tile), jnp.float32)
        for r in range(rows):
            here = fields[k, r]
            above = fields[k, r - 1] if r > 0 else none
            below = fields[k, r + 1] if r < rows - 1 else none
            left = jnp.where(sublane == 0, 0.0, pltpu.roll(here, 1, 0))
            right = jnp.where(sublane == cols - 1, 0.0, pltpu.roll(here, cols - 1, 0))
            chosen[0, r] = here
            for s in range(slots - 1):
                code = code_table[s, r]
                chosen[s + 1, r] = jnp.where(
                    code < 1.5,
                    jnp.where(code < 0.5, above, below),
                    jnp.where(code < 2.5, left, right),
                )

    def inside(k, first):
        shift = shifts_ref[order_ref[k]]
        choose(k)

        @pl.loop(0, rows)
        def _(r):
            if first:
                for c in range(cols):
                    load(r, c).wait()
            for c in range(cols):
                total = blocks[r, c, 0] * chosen[0, r, c : c + 1]
                for s in range(1, slots):
                    total = total + blocks[r, c, s] * chosen[s, r, c : c + 1]
                product = jnp.sum(total.T, axis=0, keepdims=True)
                fields[k + 1, r, c : c + 1] = product - shift * chosen[0, r, c : c + 1]

    def pick(r, c, direction):
        total = jnp.zeros((tile, tile), jnp.float32)
        for s in range(slots - 1):
            code = code_table[s, r, c : c + 1]
            total = jnp.where(code == float(direction), blocks[r, c, s + 1], total)
        return total

    def gather_rim():
        for side in range(2):
            @pl.loop(0, cols)
            def _(c, side=side):
                total = jnp.zeros((tile, tile), jnp.float32)
                for s in range(slots - 1):
                    code = code_table[s, side * (rows - 1), pl.ds(c, 1)]
                    total = jnp.where(
                        code == float(side), blocks[side * (rows - 1), c, s + 1], total
                    )
                rim_rows[side, c] = total

            @pl.loop(0, rows)
            def _(r, side=side):
                rim_cols[side, r] = pick(r, side * (cols - 1), side + LEFT)

    def rim(k):
        for r in range(rows):
            for c in range(cols):
                parts = []
                for side in range(2):
                    if r == side * (rows - 1):
                        parts.append(rim_rows[side, c] * halo_rows[k, side, c : c + 1])
                    if c == side * (cols - 1):
                        parts.append(rim_cols[side, r] * halo_cols[k, side, r : r + 1])
                if parts:
                    product = jnp.sum(sum(parts[1:], parts[0]).T, axis=0, keepdims=True)
                    fields[k + 1, r, c : c + 1] += product

    def edges(k):
        for r in range(rows):
            edge_cols[k, 0, r : r + 1] = fields[k, r, 0:1]
            edge_cols[k, 1, r : r + 1] = fields[k, r, cols - 1 : cols]

    pairs = prev + basis
    per_line = tile // pitch
    pair_lane = lax.broadcasted_iota(jnp.int32, (pairs, tile), 1)
    pair_index = lax.broadcasted_iota(jnp.int32, (pairs, tile), 0)
    line_index = lax.broadcasted_iota(jnp.int32, stats.shape, 0)

    def inner(k):
        field = fields[k + 1]
        values = []
        for g in range(groups_prev + 1):
            if g < groups_prev:
                other = earlier[g * basis : (g + 1) * basis]
            else:
                other = fields[1 : basis + 1]
            values.append(jnp.sum(jnp.sum(other * field[None], axis=1), axis=1))
        value = jnp.sum(jnp.concatenate(values, axis=0), axis=1, keepdims=True)
        line = jnp.sum(
            jnp.where(pair_lane == (k % per_line) * pitch + pair_index, value, 0.0),
            axis=0,
            keepdims=True,
        )
        stats[...] += jnp.where(line_index == k // per_line, line, 0.0)

    small[0].wait()
    small[1].wait()
    start = weights_ref[0] * earlier[0]
    for p in range(1, prev):
        start = start + weights_ref[p] * earlier[p]
    fields[0] = start
    edges(0)
    for copy in small[2:]:
        copy.wait()
    for s, lines in enumerate(code_columns()):
        for r, line in enumerate(lines):
            code_table[s, r] = line
    pl.semaphore_wait(barrier, peers - 1)
    send(0, (ABOVE, BELOW, LEFT, RIGHT))
    inside(0, True)
    gather_rim()

    @pl.loop(0, basis - 1)
    def _(k):
        receive(k)
        rim(k)
        edges(k + 1)
        send(k + 1, (ABOVE, BELOW, LEFT, RIGHT))
        inside(k + 1, False)
        inner(k)

    receive(basis - 1)
    rim(basis - 1)
    inner(basis - 1)

    def deliver(d):
        return pltpu.make_async_remote_copy(
            src_ref=stats,
            dst_ref=gathered.at[me],
            send_sem=all_send.at[d],
            recv_sem=all_recv.at[me],
            device_id=place((me + d) % peers),
            device_id_type=MESH,
        )

    @pl.loop(1, peers)
    def _(d):
        deliver(d).start()

    gathered[me] = stats[...]

    @pl.loop(1, peers)
    def _(d):
        source = (me + d) % peers
        pltpu.make_async_copy(
            gathered.at[source], gathered.at[source], all_recv.at[source]
        ).wait()

    total = jnp.sum(gathered[...], axis=0) * (1.0 / cells)
    turned = total.T
    proj = [None] * pairs
    for k in range(basis):
        for g in range(groups_prev + 1):
            first = (k % per_line) * pitch + g * basis
            column = turned[first : first + basis, k // per_line : k // per_line + 1]
            column = jnp.broadcast_to(column, (basis, tile))
            spread[g * basis + k] = column
            proj[g * basis + k] = column
        first = (k % per_line) * pitch
        proj_ref[k : k + 1, :] = total[k // per_line : k // per_line + 1, first : first + prev]

    for k in range(basis):
        value = fields[k + 1]
        for p in range(prev):
            g, q = p // basis, p % basis
            value = value - spread[g * basis + k, q : q + 1][None] * earlier[p]
        basis_ref[k] = value

    gram = {}
    for j in range(basis):
        for k in range(j, basis):
            removed = proj[j] * proj[k]
            for g in range(1, groups_prev):
                removed = removed + proj[g * basis + j] * proj[g * basis + k]
            gram[j, k] = spread[groups_prev * basis + k, j : j + 1] - jnp.sum(
                removed, axis=0, keepdims=True
            )
    lower, inverse = {}, []
    for j in range(basis):
        root = jnp.sqrt(gram[j, j])
        inverse.append(1.0 / root)
        lower[j, j] = root
        for k in range(j + 1, basis):
            lower[k, j] = gram[j, k] * inverse[j]
        for k in range(j + 1, basis):
            for m in range(k, basis):
                gram[k, m] = gram[k, m] - lower[k, j] * lower[m, j]

    row_index = lax.broadcasted_iota(jnp.int32, (basis, tile), 0)
    upper = jnp.zeros((basis, tile), jnp.float32)
    for j in range(basis):
        line = jnp.zeros((1, tile), jnp.float32)
        for k in range(j, basis):
            line = jnp.where(lane[0:1] == k, lower[k, j], line)
        upper = jnp.where(row_index == j, line, upper)
    upper_ref[...] = upper[:, :basis]

    for r in range(rows):
        done = []
        for k in range(basis):
            value = basis_ref[k, r]
            for j in range(k):
                value = value - lower[k, j] * done[j]
            value = value * inverse[k]
            done.append(value)
            basis_ref[k, r] = value

    @pl.loop(0, basis)
    def _(k):
        for direction in range(4):
            @pl.when(has[direction])
            def _(direction=direction):
                hop(k, direction).wait_send()

    @pl.loop(1, peers)
    def _(d):
        deliver(d).wait_send()


def shards(n_rows, n_cols, tile_blocks, tile_codes, shifts, shift_order, earlier, start_weights):
    rows, cols, slots, tile, _ = tile_blocks.shape
    basis, prev = shifts.shape[0], earlier.shape[0]
    peers = n_rows * n_cols
    pitch = pl.next_power_of_2(prev + basis)
    lines = pl.cdiv(basis, tile // pitch)
    vmem = pl.BlockSpec(memory_space=pltpu.VMEM)
    hbm = pl.BlockSpec(memory_space=pltpu.HBM)
    codes = jnp.transpose(tile_codes, (2, 0, 1))
    f32 = jnp.float32
    basis_out, upper, proj = pl.pallas_call(
        functools.partial(kernel, n_rows, n_cols, pitch),
        out_shape=(
            jax.ShapeDtypeStruct((basis, rows, cols, tile), f32),
            jax.ShapeDtypeStruct((basis, basis), f32),
            jax.ShapeDtypeStruct((basis, prev), f32),
        ),
        in_specs=[hbm] * 6,
        out_specs=(vmem, vmem, vmem),
        scratch_shapes=[
            pltpu.VMEM(tile_blocks.shape, f32),
            pltpu.VMEM(earlier.shape, f32),
            pltpu.VMEM(codes.shape, jnp.int32),
            pltpu.SMEM(shifts.shape, f32),
            pltpu.SMEM(shift_order.shape, jnp.int32),
            pltpu.SMEM(start_weights.shape, f32),
            pltpu.VMEM((basis + 1, rows, cols, tile), f32),
            pltpu.VMEM((slots, rows, cols, tile), f32),
            pltpu.VMEM((basis, 2, cols, tile), f32),
            pltpu.VMEM((basis, 2, rows, tile), f32),
            pltpu.VMEM((basis, 2, rows, tile), f32),
            pltpu.VMEM((2, cols, tile, tile), f32),
            pltpu.VMEM((2, rows, tile, tile), f32),
            pltpu.VMEM((slots - 1, rows, cols, tile), f32),
            pltpu.VMEM((lines, tile), f32),
            pltpu.VMEM((peers, lines, tile), f32),
            pltpu.VMEM(((prev // basis + 1) * basis, basis, tile), f32),
            pltpu.SemaphoreType.DMA((rows, cols)),
            pltpu.SemaphoreType.DMA((5,)),
            pltpu.SemaphoreType.DMA((basis, 4)),
            pltpu.SemaphoreType.DMA((basis, 4)),
            pltpu.SemaphoreType.DMA((peers,)),
            pltpu.SemaphoreType.DMA((peers,)),
        ],
        compiler_params=pltpu.CompilerParams(
            collective_id=0, has_side_effects=True, vmem_limit_bytes=48 * 1024 * 1024
        ),
        name="sstep",
    )(*[pltpu.with_memory_space_constraint(x, pltpu.HBM) for x in (tile_blocks, codes, shifts, shift_order, earlier, start_weights)])
    return basis_out, upper, proj.T


def solution(mesh):
    in_specs = (
        P(("groups", "rows"), "cols", None, None, None),
        P(("groups", "rows"), "cols", None),
        P("groups"),
        P("groups"),
        P(None, ("groups", "rows"), "cols", None),
        P("groups"),
    )
    out_specs = (P(None, ("groups", "rows"), "cols", None), P("groups", None), P("groups", None))
    body = functools.partial(shards, mesh.shape["rows"], mesh.shape["cols"])
    return jax.shard_map(body, mesh=mesh, in_specs=in_specs, out_specs=out_specs, check_vma=False)
```

profile of v0, /device:TPU:0, one launch (start us, length us, event | category | flops | bytes accessed | tf_op | source)
XLA Modules:
  0.0 39.4 jit_solution(5764709644733803285)
XLA Ops:
  0.6 36.9 %sstep.1 = (f32[8,4,8,128]{3,2,1,0:T(8,128)S(1)}, f32[8,8]{1,0:T(8,128)S(1)}, f32[8,16]{1,0:T(8,128)S(1)}) custom-call(f32[4,8,4,128,128]{4,3,2,1,0:T(8,128)} %blocks_hbm.1, s32[3,4,8]{2,1,0:T(4,128)} %bitcast.3, f32[8]{0:T(128)} %shifts_hbm.1, s32[8]{0:T(128)} %order_hbm.1, f32[16,4,8,128]{3,2,1,0:T(8,128)} %earlier_hbm.1, f32[16]{0:T(128)} %weights_hbm.1), custom_call_target="tpu_custom_call" | custom-call | tf_op jit(solution)/shard_map/sstep/pallas_call | solution.py:374
  37.6 0.7 %copy.12 = f32[8,4,8,128]{3,2,1,0:T(8,128)} copy(f32[8,4,8,128]{3,2,1,0:T(8,128)S(1)} %get-tuple-element.12) | data formatting | bytes 262144
  38.2 0.6 %copy.13 = f32[8,8]{1,0:T(8,128)} copy(f32[8,8]{1,0:T(8,128)S(1)} %get-tuple-element.13) | data formatting | bytes 512
  38.8 0.6 %copy.14 = f32[16,8]{0,1:T(8,128)} copy(f32[16,8]{0,1:T(8,128)S(1)} %bitcast.2) | data formatting | bytes 1024
where the time goes:
time: 39.6 us; the launch traced here: 39.4 us
  Pallas kernels  36.9 us (93%)
  local copies, waits for them, and re-layouts  1.84 us (5%)
  between operations  0.64 us (2%)
    pallas_call x1, Pallas kernels, shards(): pl.pallas_call(functools.partial(kernel, n_rows, n_cols, pitch), out_shap...  36.9 us
    unnamed x3, local copies, waits for them, and re-layouts  1.84 us

commit v1 on v0

--- a/solution.py
+++ b/solution.py
@@ -359,6 +359,19 @@
     @pl.loop(1, peers)
     def _(d):
         deliver(d).wait_send()
+
+
+def store(basis_ref, upper_ref, proj_ref, basis_hbm, upper_hbm, proj_hbm, sem):
+    copies = [
+        pltpu.make_async_copy(src, dst, sem.at[i])
+        for i, (src, dst) in enumerate(
+            [(basis_ref, basis_hbm), (upper_ref, upper_hbm), (proj_ref, proj_hbm)]
+        )
+    ]
+    for copy in copies:
+        copy.start()
+    for copy in copies:
+        copy.wait()
 
 
 def shards(n_rows, n_cols, tile_blocks, tile_codes, shifts, shift_order, earlier, start_weights):
@@ -410,6 +423,15 @@
         ),
         name="sstep",
     )(*[pltpu.with_memory_space_constraint(x, pltpu.HBM) for x in (tile_blocks, codes, shifts, shift_order, earlier, start_weights)])
+    results = (basis_out, upper, proj)
+    basis_out, upper, proj = pl.pallas_call(
+        store,
+        out_shape=tuple(jax.ShapeDtypeStruct(x.shape, f32) for x in results),
+        in_specs=[vmem] * 3,
+        out_specs=(hbm,) * 3,
+        scratch_shapes=[pltpu.SemaphoreType.DMA((3,))],
+        name="store",
+    )(*[pltpu.with_memory_space_constraint(x, pltpu.VMEM) for x in results])
     return basis_out, upper, proj.T
 
 

time: 39.6 us -> 38.4 us (0.970)
  local copies, waits for them, and re-layouts: 1.84 us -> 0 us
  Pallas kernels: 36.9 us -> 37.6 us
    unnamed x3 -> x0, local copies, waits for them, and re-layouts: 1.84 us -> none
    pallas_call x0 -> x1, Pallas kernels: none -> 0.69 us  [shards(): pl.pallas_call(store, out_shape=tuple((jax.ShapeDtypeStruct(x.shape, f32)...]
where the time goes in v1:
time: 38.4 us; the launch traced here: 38.3 us
  Pallas kernels  37.6 us (98%)
  between operations  0.64 us (2%)
    pallas_call x1, Pallas kernels, shards(): pl.pallas_call(functools.partial(kernel, n_rows, n_cols, pitch), out_shap...  36.9 us

profile of v1, /device:TPU:0, one launch (start us, length us, event | category | flops | bytes accessed | tf_op | source)
XLA Modules:
  0.0 38.3 jit_solution(10064348337448524496)
XLA Ops:
  0.6 36.9 %sstep.1 = (f32[8,4,8,128]{3,2,1,0:T(8,128)S(1)}, f32[8,8]{1,0:T(8,128)S(1)}, f32[8,16]{1,0:T(8,128)S(1)}) custom-call(f32[4,8,4,128,128]{4,3,2,1,0:T(8,128)} %blocks_hbm.1, s32[3,4,8]{2,1,0:T(4,128)} %bitcast.2, f32[8]{0:T(128)} %shifts_hbm.1, s32[8]{0:T(128)} %order_hbm.1, f32[16,4,8,128]{3,2,1,0:T(8,128)} %earlier_hbm.1, f32[16]{0:T(128)} %weights_hbm.1), custom_call_target="tpu_custom_call" | custom-call | tf_op jit(solution)/shard_map/sstep/pallas_call | solution.py:387
  37.6 0.7 %store.1 = (f32[8,4,8,128]{3,2,1,0:T(8,128)}, f32[8,8]{1,0:T(8,128)}, f32[8,16]{1,0:T(8,128)}) custom-call(f32[8,4,8,128]{3,2,1,0:T(8,128)S(1)} %get-tuple-element.9.basis_ref, f32[8,8]{1,0:T(8,128)S(1)} %get-tuple-element.10.upper_ref, f32[8,16]{1,0:T(8,128)S(1)} %get-tuple-element.11.proj_ref), custom_call_target="tpu_custom_call" | custom-call | tf_op jit(solution)/shard_map/store/pallas_call | solution.py:427

commit v2 on v1

--- a/solution.py
+++ b/solution.py
@@ -16,7 +16,7 @@
     blocks_hbm, codes_hbm, shifts_hbm, order_hbm, earlier_hbm, weights_hbm,
     basis_ref, upper_ref, proj_ref,
     blocks, earlier, codes_ref, shifts_ref, order_ref, weights_ref,
-    fields, chosen, halo_rows, halo_cols, edge_cols, rim_rows, rim_cols,
+    fields, chosen, packed, rim_packed, halo_rows, halo_cols, edge_cols, rim_rows, rim_cols,
     code_table, stats, gathered, spread,
     load_sem, small_sem, send_sem, recv_sem, all_send, all_recv,
 ):
@@ -88,9 +88,9 @@
 
     def hop(k, direction):
         if direction == ABOVE:
-            src, dst, where_to = fields.at[k, 0], halo_rows.at[k, 1], {"rows": my_row - 1}
+            src, dst, where_to = packed.at[k, 0], halo_rows.at[k, 1], {"rows": my_row - 1}
         elif direction == BELOW:
-            src, dst, where_to = fields.at[k, rows - 1], halo_rows.at[k, 0], {"rows": my_row + 1}
+            src, dst, where_to = packed.at[k, 1], halo_rows.at[k, 0], {"rows": my_row + 1}
         elif direction == LEFT:
             src, dst, where_to = edge_cols.at[k, 0], halo_cols.at[k, 1], {"cols": my_col - 1}
         else:
@@ -117,8 +117,8 @@
             def _(direction=direction):
                 hop(k, direction).start()
 
-    def receive(k):
-        for direction in range(4):
+    def receive(k, directions):
+        for direction in directions:
             @pl.when(has[direction])
             def _(direction=direction):
                 arrival(k, direction).wait()
@@ -128,6 +128,10 @@
     diagonal = lax.broadcasted_iota(jnp.int32, (cols, cols), 0) == lax.broadcasted_iota(
         jnp.int32, (cols, cols), 1
     )
+
+    lane_index = lax.broadcasted_iota(jnp.int32, (cols, tile), 1)
+    offset = lane_index % cols - sublane
+    n_parts = tile // cols
 
     def code_columns():
         codes = codes_ref[...].astype(jnp.float32)
@@ -196,18 +200,90 @@
             def _(r, side=side):
                 rim_cols[side, r] = pick(r, side * (cols - 1), side + LEFT)
 
-    def rim(k):
+    def rim(k, with_rows):
         for r in range(rows):
             for c in range(cols):
                 parts = []
                 for side in range(2):
-                    if r == side * (rows - 1):
+                    if with_rows and r == side * (rows - 1):
                         parts.append(rim_rows[side, c] * halo_rows[k, side, c : c + 1])
                     if c == side * (cols - 1):
                         parts.append(rim_cols[side, r] * halo_cols[k, side, r : r + 1])
                 if parts:
                     product = jnp.sum(sum(parts[1:], parts[0]).T, axis=0, keepdims=True)
                     fields[k + 1, r, c : c + 1] += product
+
+    def repack(block):
+        total = jnp.where(offset == 0, block, 0.0)
+        for shift in range(1, cols):
+            turned = pltpu.roll(block, cols - shift, 0)
+            total = jnp.where(offset == shift, pltpu.roll(turned, shift, 1), total)
+            total = jnp.where(
+                offset == shift - cols, pltpu.roll(turned, tile + shift - cols, 1), total
+            )
+        return total
+
+    def pack_rim():
+        for side in range(2):
+            @pl.loop(0, n_parts // 4)
+            def _(step, side=side):
+                for part in range(4):
+                    index = step * 4 + part
+                    line = [
+                        rim_rows[side, c, pl.ds(index * cols, cols)] for c in range(cols)
+                    ]
+                    bit = 1
+                    while bit < cols:
+                        low = (lane_index & bit) == 0
+                        for c in range(cols):
+                            if c & bit == 0:
+                                a, b = line[c], line[c | bit]
+                                line[c] = jnp.where(low, a, pltpu.roll(b, bit, 1))
+                                line[c | bit] = jnp.where(low, pltpu.roll(a, tile - bit, 1), b)
+                        bit *= 2
+                    for c in range(cols):
+                        rim_packed[side, c, index] = line[c]
+
+            @pl.loop(0, cols)
+            def _(c, side=side):
+                line = [rim_packed[side, c, part] for part in range(n_parts)]
+                bit = 1
+                while bit < n_parts:
+                    high = ((lane_index // cols) & bit) != 0
+                    line = [
+                        jnp.where(high, line[(part + bit) % n_parts], line[part])
+                        for part in range(n_parts)
+                    ]
+                    bit *= 2
+                for part in range(n_parts):
+                    rim_packed[side, c, part] = line[part]
+
+    def rim_line(k, side, inner_part):
+        rows_in = [halo_rows[k, side, c : c + 1] for c in range(cols)]
+        sums = [inner_part]
+        for part in range(n_parts):
+            total = rim_packed[side, 0, part] * rows_in[0]
+            for c in range(1, cols):
+                total = total + rim_packed[side, c, part] * rows_in[c]
+            sums.append(pltpu.roll(total, part * cols, 1) if part else total)
+        while len(sums) > 1:
+            sums = [sum(sums[i + 1 : i + 2], sums[i]) for i in range(0, len(sums), 2)]
+        return sums[0]
+
+    def finish(k, last):
+        receive(k, (LEFT, RIGHT))
+        rim(k, False)
+        inner_parts = [repack(fields[k + 1, side * (rows - 1)]) for side in range(2)]
+        for side in range(2):
+            receive(k, (side,))
+            packed[k + 1, side] = rim_line(k, side, inner_parts[side])
+            if not last:
+                send(k + 1, (side,))
+        for side in range(2):
+            fields[k + 1, side * (rows - 1)] = repack(packed[k + 1, side])
+        if not last:
+            edges(k + 1)
+            send(k + 1, (LEFT, RIGHT))
 
     def edges(k):
         for r in range(rows):
@@ -243,6 +319,8 @@
     for p in range(1, prev):
         start = start + weights_ref[p] * earlier[p]
     fields[0] = start
+    for side in range(2):
+        packed[0, side] = fields[0, side * (rows - 1)]
     edges(0)
     for copy in small[2:]:
         copy.wait()
@@ -254,17 +332,23 @@
     inside(0, True)
     gather_rim()
 
-    @pl.loop(0, basis - 1)
+    receive(0, range(4))
+    rim(0, True)
+    for side in range(2):
+        packed[1, side] = repack(fields[1, side * (rows - 1)])
+    edges(1)
+    send(1, range(4))
+    inside(1, False)
+    pack_rim()
+    inner(0)
+
+    @pl.loop(1, basis - 1)
     def _(k):
-        receive(k)
-        rim(k)
-        edges(k + 1)
-        send(k + 1, (ABOVE, BELOW, LEFT, RIGHT))
+        finish(k, False)
         inside(k + 1, False)
         inner(k)
 
-    receive(basis - 1)
-    rim(basis - 1)
+    finish(basis - 1, True)
     inner(basis - 1)
 
     def deliver(d):
@@ -402,6 +486,8 @@
             pltpu.SMEM(start_weights.shape, f32),
             pltpu.VMEM((basis + 1, rows, cols, tile), f32),
             pltpu.VMEM((slots, rows, cols, tile), f32),
+            pltpu.VMEM((basis + 1, 2, cols, tile), f32),
+            pltpu.VMEM((2, cols, tile // cols, cols, tile), f32),
             pltpu.VMEM((basis, 2, cols, tile), f32),
             pltpu.VMEM((basis, 2, rows, tile), f32),
             pltpu.VMEM((basis, 2, rows, tile), f32),

time: 38.4 us -> 37.6 us (0.979)
  Pallas kernels: 37.6 us -> 36.8 us
    pallas_call x1, Pallas kernels: 36.9 us -> 36.1 us  [shards(): pl.pallas_call(functools.partial(kernel, n_rows, n_cols, pitch), out_shap...]
where the time goes in v2:
time: 37.6 us; the launch traced here: 37.4 us
  Pallas kernels  36.8 us (98%)
  between operations  0.64 us (2%)
    pallas_call x1, Pallas kernels, shards(): pl.pallas_call(functools.partial(kernel, n_rows, n_cols, pitch), out_shap...  36.1 us

profile of v2, /device:TPU:0, one launch (start us, length us, event | category | flops | bytes accessed | tf_op | source)
XLA Modules:
  0.0 37.4 jit_solution(7715192948241253778)
XLA Ops:
  0.6 36.1 %sstep.1 = (f32[8,4,8,128]{3,2,1,0:T(8,128)S(1)}, f32[8,8]{1,0:T(8,128)S(1)}, f32[8,16]{1,0:T(8,128)S(1)}) custom-call(f32[4,8,4,128,128]{4,3,2,1,0:T(8,128)} %blocks_hbm.1, s32[3,4,8]{2,1,0:T(4,128)} %bitcast.2, f32[8]{0:T(128)} %shifts_hbm.1, s32[8]{0:T(128)} %order_hbm.1, f32[16,4,8,128]{3,2,1,0:T(8,128)} %earlier_hbm.1, f32[16]{0:T(128)} %weights_hbm.1), custom_call_target="tpu_custom_call" | custom-call | tf_op jit(solution)/shard_map/sstep/pallas_call | solution.py:471
  36.8 0.7 %store.1 = (f32[8,4,8,128]{3,2,1,0:T(8,128)}, f32[8,8]{1,0:T(8,128)}, f32[8,16]{1,0:T(8,128)}) custom-call(f32[8,4,8,128]{3,2,1,0:T(8,128)S(1)} %get-tuple-element.9.basis_ref, f32[8,8]{1,0:T(8,128)S(1)} %get-tuple-element.10.upper_ref, f32[8,16]{1,0:T(8,128)S(1)} %get-tuple-element.11.proj_ref), custom_call_target="tpu_custom_call" | custom-call | tf_op jit(solution)/shard_map/store/pallas_call | solution.py:513

commit v3 on v1

--- a/solution.py
+++ b/solution.py
@@ -16,9 +16,9 @@
     blocks_hbm, codes_hbm, shifts_hbm, order_hbm, earlier_hbm, weights_hbm,
     basis_ref, upper_ref, proj_ref,
     blocks, earlier, codes_ref, shifts_ref, order_ref, weights_ref,
-    fields, chosen, halo_rows, halo_cols, edge_cols, rim_rows, rim_cols,
-    code_table, stats, gathered, spread,
-    load_sem, small_sem, send_sem, recv_sem, all_send, all_recv,
+    fields, chosen, packed, cross, rim_packed, halo_rows, halo_cols, first_cols, edge_cols, rim_tiles,
+    code_table, stats, gathered, late, late_gathered, spread,
+    load_sem, small_sem, send_sem, recv_sem, all_sem,
 ):
     rows, cols, slots, tile, _ = blocks.shape
     basis = basis_ref.shape[0]
@@ -28,6 +28,13 @@
     cells = float(peers * rows * cols * tile)
     my_row, my_col = lax.axis_index("rows"), lax.axis_index("cols")
     me = my_row * n_cols + my_col
+
+    barrier = pltpu.get_barrier_semaphore()
+    all_rows = [lax.rem(my_row + d, n_rows) for d in range(n_rows)]
+    all_cols = [lax.rem(my_col + d, n_cols) for d in range(n_cols)]
+    others = [{"rows": r, "cols": c} for r in all_rows for c in all_cols][1:]
+    for other in others:
+        pl.semaphore_signal(barrier, inc=1, device_id=other, device_id_type=MESH)
 
     def load(r, c):
         return pltpu.make_async_copy(
@@ -52,22 +59,11 @@
         for c in range(cols):
             load(r, c).start()
 
-    barrier = pltpu.get_barrier_semaphore()
-
-    def place(index):
-        return {"rows": index // n_cols, "cols": index % n_cols}
-
-    @pl.loop(1, peers)
-    def _(d):
-        pl.semaphore_signal(
-            barrier, inc=1, device_id=place((me + d) % peers), device_id_type=MESH
-        )
-
     for k in range(1, basis + 1):
         fields[k] = jnp.zeros((rows, cols, tile), jnp.float32)
     stats[...] = jnp.zeros_like(stats)
     no_row = jnp.zeros((basis, cols, tile), jnp.float32)
-    no_col = jnp.zeros((basis, rows, tile), jnp.float32)
+    no_first = jnp.zeros((rows, tile), jnp.float32)
     has = [my_row > 0, my_row < n_rows - 1, my_col > 0, my_col < n_cols - 1]
 
     @pl.when(my_row == 0)
@@ -80,21 +76,26 @@
 
     @pl.when(my_col == 0)
     def _():
-        halo_cols[:, 0] = no_col
+        halo_cols[:, 0] = no_row
+        first_cols[0] = no_first
 
     @pl.when(my_col == n_cols - 1)
     def _():
-        halo_cols[:, 1] = no_col
-
-    def hop(k, direction):
+        halo_cols[:, 1] = no_row
+        first_cols[1] = no_first
+
+    def hop(k, direction, first=False):
         if direction == ABOVE:
-            src, dst, where_to = fields.at[k, 0], halo_rows.at[k, 1], {"rows": my_row - 1}
+            src, dst, where_to = packed.at[k, 0], halo_rows.at[k, 1], {"rows": my_row - 1}
         elif direction == BELOW:
-            src, dst, where_to = fields.at[k, rows - 1], halo_rows.at[k, 0], {"rows": my_row + 1}
-        elif direction == LEFT:
-            src, dst, where_to = edge_cols.at[k, 0], halo_cols.at[k, 1], {"cols": my_col - 1}
+            src, dst, where_to = packed.at[k, rows - 1], halo_rows.at[k, 0], {"rows": my_row + 1}
         else:
-            src, dst, where_to = edge_cols.at[k, 1], halo_cols.at[k, 0], {"cols": my_col + 1}
+            side = direction - LEFT
+            where_to = {"cols": my_col + 2 * side - 1}
+            if first:
+                src, dst = edge_cols.at[side], first_cols.at[1 - side]
+            else:
+                src, dst = cross.at[k], halo_cols.at[k, 1 - side]
         return pltpu.make_async_remote_copy(
             src_ref=src,
             dst_ref=dst,
@@ -104,30 +105,37 @@
             device_id_type=MESH,
         )
 
-    def arrival(k, direction):
+    def arrival(k, direction, first):
         if direction in (ABOVE, BELOW):
             dst = halo_rows.at[k, direction]
+        elif first:
+            dst = first_cols.at[direction - LEFT]
         else:
-            dst = halo_cols.at[k, direction - 2]
+            dst = halo_cols.at[k, direction - LEFT]
         return pltpu.make_async_copy(dst, dst, recv_sem.at[k, direction])
 
-    def send(k, directions):
+    def send(k, directions, first=False):
         for direction in directions:
             @pl.when(has[direction])
             def _(direction=direction):
-                hop(k, direction).start()
-
-    def receive(k):
-        for direction in range(4):
+                hop(k, direction, first).start()
+
+    def receive(k, directions, first=False):
+        for direction in directions:
             @pl.when(has[direction])
             def _(direction=direction):
-                arrival(k, direction).wait()
+                arrival(k, direction, first).wait()
 
     sublane = lax.broadcasted_iota(jnp.int32, (cols, tile), 0)
     lane = lax.broadcasted_iota(jnp.int32, (basis, tile), 1)
     diagonal = lax.broadcasted_iota(jnp.int32, (cols, cols), 0) == lax.broadcasted_iota(
         jnp.int32, (cols, cols), 1
     )
+
+    lane_index = lax.broadcasted_iota(jnp.int32, (cols, tile), 1)
+    within = lane_index % cols
+    offset = within - sublane
+    n_parts = tile // cols
 
     def code_columns():
         codes = codes_ref[...].astype(jnp.float32)
@@ -190,29 +198,139 @@
                     total = jnp.where(
                         code == float(side), blocks[side * (rows - 1), c, s + 1], total
                     )
-                rim_rows[side, c] = total
+                rim_tiles[side, c] = total
 
             @pl.loop(0, rows)
             def _(r, side=side):
-                rim_cols[side, r] = pick(r, side * (cols - 1), side + LEFT)
-
-    def rim(k):
+                rim_tiles[2, side * rows + r] = pick(r, side * (cols - 1), side + LEFT)
+
+    def rim():
         for r in range(rows):
             for c in range(cols):
                 parts = []
                 for side in range(2):
                     if r == side * (rows - 1):
-                        parts.append(rim_rows[side, c] * halo_rows[k, side, c : c + 1])
+                        parts.append(rim_tiles[side, c] * halo_rows[0, side, c : c + 1])
                     if c == side * (cols - 1):
-                        parts.append(rim_cols[side, r] * halo_cols[k, side, r : r + 1])
+                        parts.append(
+                            rim_tiles[2, side * rows + r] * first_cols[side, r : r + 1]
+                        )
                 if parts:
                     product = jnp.sum(sum(parts[1:], parts[0]).T, axis=0, keepdims=True)
-                    fields[k + 1, r, c : c + 1] += product
-
-    def edges(k):
+                    fields[1, r, c : c + 1] += product
+
+    def repack(block):
+        total = jnp.where(offset == 0, block, 0.0)
+        for shift in range(1, cols):
+            turned = pltpu.roll(block, cols - shift, 0)
+            total = jnp.where(offset == shift, pltpu.roll(turned, shift, 1), total)
+            total = jnp.where(
+                offset == shift - cols, pltpu.roll(turned, tile + shift - cols, 1), total
+            )
+        return total
+
+    def pack_rim():
+        @pl.loop(0, 3)
+        def _(group):
+            bit = 1
+            while bit < cols:
+                low = (lane_index & bit) == 0
+                for part in range(n_parts):
+                    for c in range(cols):
+                        if c & bit == 0:
+                            if bit == 1:
+                                a, b = (
+                                    rim_tiles[group, i, part * cols : (part + 1) * cols]
+                                    for i in (c, c | bit)
+                                )
+                            else:
+                                a, b = (rim_packed[group, i, part] for i in (c, c | bit))
+                            rim_packed[group, c, part] = jnp.where(low, a, pltpu.roll(b, bit, 1))
+                            rim_packed[group, c | bit, part] = jnp.where(
+                                low, pltpu.roll(a, tile - bit, 1), b
+                            )
+                bit *= 2
+
+            @pl.loop(0, cols)
+            def _(c):
+                line = [rim_packed[group, c, part] for part in range(n_parts)]
+                bit = 1
+                while bit < n_parts:
+                    high = ((lane_index // cols) & bit) != 0
+                    line = [
+                        jnp.where(high, line[(part + bit) % n_parts], line[part])
+                        for part in range(n_parts)
+                    ]
+                    bit *= 2
+                for part in range(n_parts):
+                    rim_packed[group, c, part] = line[part]
+
+    def turn(block, shift):
+        return pltpu.roll(block, shift % tile, 1) if shift % tile else block
+
+    def rim_line(group, rows_in, sums):
+        for part in range(n_parts):
+            total = rim_packed[group, 0, part] * rows_in[0]
+            for c in range(1, cols):
+                total = total + rim_packed[group, c, part] * rows_in[c]
+            sums = sums + [turn(total, part * cols)]
+        while len(sums) > 1:
+            sums = [sum(sums[i + 1 : i + 2], sums[i]) for i in range(0, len(sums), 2)]
+        return sums[0]
+
+    def crossing(lines, total):
+        for r, block in lines:
+            total = jnp.where(within == rows + r, turn(block, rows + r), total)
+            total = jnp.where(within == r, turn(block, r + 1 - cols), total)
+        return total
+
+    middle = range(1, rows - 1)
+    outer = [0, rows - 1]
+    nothing = jnp.zeros((cols, tile), jnp.float32)
+
+    def finish(k, last):
+        parts = [repack(fields[k + 1, r]) for r in range(rows)]
+        receive(k, (LEFT, RIGHT))
+        line = rim_line(
+            2,
+            [
+                jnp.where(within < rows, halo_cols[k, 0, c : c + 1], halo_cols[k, 1, c : c + 1])
+                for c in range(cols)
+            ],
+            [],
+        )
         for r in range(rows):
-            edge_cols[k, 0, r : r + 1] = fields[k, r, 0:1]
-            edge_cols[k, 1, r : r + 1] = fields[k, r, cols - 1 : cols]
+            parts[r] = parts[r] + jnp.where(
+                within == 0,
+                turn(line, -r),
+                jnp.where(within == cols - 1, turn(line, cols - 1 - rows - r), 0.0),
+            )
+        for r in middle:
+            fields[k + 1, r] = repack(parts[r])
+        if last:
+            known = products(k, middle)
+        else:
+            known = crossing([(r, parts[r]) for r in middle], nothing)
+        receive(k, (ABOVE, BELOW))
+        for side, r in enumerate(outer):
+            parts[r] = rim_line(
+                side, [halo_rows[k, side, c : c + 1] for c in range(cols)], [parts[r]]
+            )
+            if not last:
+                packed[k + 1, r] = parts[r]
+        if not last:
+            send(k + 1, (ABOVE, BELOW))
+            cross[k + 1] = crossing([(r, parts[r]) for r in outer], known)
+            send(k + 1, (LEFT, RIGHT))
+        for r in outer:
+            fields[k + 1, r] = repack(parts[r])
+        if last:
+            late[...] = line_of(known + products(k, outer), 0)
+
+    def edges():
+        for r in range(rows):
+            edge_cols[0, r : r + 1] = fields[0, r, 0:1]
+            edge_cols[1, r : r + 1] = fields[0, r, cols - 1 : cols]
 
     pairs = prev + basis
     per_line = tile // pitch
@@ -220,21 +338,31 @@
     pair_index = lax.broadcasted_iota(jnp.int32, (pairs, tile), 0)
     line_index = lax.broadcasted_iota(jnp.int32, stats.shape, 0)
 
-    def inner(k):
-        field = fields[k + 1]
+    def products(k, lines):
         values = []
         for g in range(groups_prev + 1):
-            if g < groups_prev:
-                other = earlier[g * basis : (g + 1) * basis]
-            else:
-                other = fields[1 : basis + 1]
-            values.append(jnp.sum(jnp.sum(other * field[None], axis=1), axis=1))
-        value = jnp.sum(jnp.concatenate(values, axis=0), axis=1, keepdims=True)
-        line = jnp.sum(
-            jnp.where(pair_lane == (k % per_line) * pitch + pair_index, value, 0.0),
-            axis=0,
-            keepdims=True,
+            total = None
+            for r in lines:
+                if g < groups_prev:
+                    other = earlier[g * basis : (g + 1) * basis, r]
+                else:
+                    other = fields[1 : basis + 1, r]
+                term = other * fields[k + 1, r][None]
+                total = term if total is None else total + term
+            values.append(jnp.sum(total, axis=1))
+        return jnp.concatenate(values, axis=0)
+
+    def inner(k):
+        record(k, products(k, range(rows)))
+
+    def line_of(values, start):
+        value = jnp.sum(values, axis=1, keepdims=True)
+        return jnp.sum(
+            jnp.where(pair_lane == start + pair_index, value, 0.0), axis=0, keepdims=True
         )
+
+    def record(k, values):
+        line = line_of(values, (k % per_line) * pitch)
         stats[...] += jnp.where(line_index == k // per_line, line, 0.0)
 
     small[0].wait()
@@ -243,57 +371,82 @@
     for p in range(1, prev):
         start = start + weights_ref[p] * earlier[p]
     fields[0] = start
-    edges(0)
+    for r in (0, rows - 1):
+        packed[0, r] = fields[0, r]
+    edges()
+    pl.semaphore_wait(barrier, peers - 1)
+    send(0, range(4), True)
     for copy in small[2:]:
         copy.wait()
     for s, lines in enumerate(code_columns()):
         for r, line in enumerate(lines):
             code_table[s, r] = line
-    pl.semaphore_wait(barrier, peers - 1)
-    send(0, (ABOVE, BELOW, LEFT, RIGHT))
     inside(0, True)
     gather_rim()
 
-    @pl.loop(0, basis - 1)
+    receive(0, range(4), True)
+    rim()
+    lines = [(r, repack(fields[1, r])) for r in range(rows)]
+    for r in (0, rows - 1):
+        packed[1, r] = lines[r][1]
+    send(1, (ABOVE, BELOW))
+    cross[1] = crossing(lines, nothing)
+    send(1, (LEFT, RIGHT))
+    inside(1, False)
+    pack_rim()
+
+    @pl.loop(1, basis - 1)
     def _(k):
-        receive(k)
-        rim(k)
-        edges(k + 1)
-        send(k + 1, (ABOVE, BELOW, LEFT, RIGHT))
+        finish(k, False)
         inside(k + 1, False)
+
+        @pl.when(k == 1)
+        def _():
+            inner(0)
+
         inner(k)
 
-    receive(basis - 1)
-    rim(basis - 1)
-    inner(basis - 1)
-
-    def deliver(d):
-        return pltpu.make_async_remote_copy(
-            src_ref=stats,
-            dst_ref=gathered.at[me],
-            send_sem=all_send.at[d],
-            recv_sem=all_recv.at[me],
-            device_id=place((me + d) % peers),
-            device_id_type=MESH,
-        )
-
-    @pl.loop(1, peers)
-    def _(d):
-        deliver(d).start()
-
+    def deliver(src, dst, send_sem, recv_sem):
+        for other in others:
+            pltpu.make_async_remote_copy(
+                src_ref=src,
+                dst_ref=dst.at[me],
+                send_sem=send_sem,
+                recv_sem=recv_sem,
+                device_id=other,
+                device_id_type=MESH,
+            ).start()
+
+    def collect(dst, sem):
+        whole = dst.at[pl.ds(0, peers - 1)]
+        pltpu.make_async_copy(whole, whole, sem).wait()
+
+    deliver(stats, gathered, all_sem.at[0], all_sem.at[1])
     gathered[me] = stats[...]
-
-    @pl.loop(1, peers)
-    def _(d):
-        source = (me + d) % peers
-        pltpu.make_async_copy(
-            gathered.at[source], gathered.at[source], all_recv.at[source]
-        ).wait()
-
+    finish(basis - 1, True)
+
+    deliver(late, late_gathered, all_sem.at[2], all_sem.at[3])
+
+    def sent(k, first):
+        for direction in range(4):
+            @pl.when(has[direction])
+            def _(direction=direction):
+                hop(k, direction, first).wait_send()
+
+    sent(0, True)
+
+    @pl.loop(1, basis)
+    def _(k):
+        sent(k, False)
+
+    late_gathered[me] = late[...]
+    collect(gathered, all_sem.at[0])
+    collect(gathered, all_sem.at[1])
+    newest = basis - 1
     total = jnp.sum(gathered[...], axis=0) * (1.0 / cells)
     turned = total.T
     proj = [None] * pairs
-    for k in range(basis):
+    for k in range(newest):
         for g in range(groups_prev + 1):
             first = (k % per_line) * pitch + g * basis
             column = turned[first : first + basis, k // per_line : k // per_line + 1]
@@ -303,32 +456,66 @@
         first = (k % per_line) * pitch
         proj_ref[k : k + 1, :] = total[k // per_line : k // per_line + 1, first : first + prev]
 
-    for k in range(basis):
+    def clean(k):
         value = fields[k + 1]
         for p in range(prev):
             g, q = p // basis, p % basis
             value = value - spread[g * basis + k, q : q + 1][None] * earlier[p]
-        basis_ref[k] = value
-
-    gram = {}
-    for j in range(basis):
-        for k in range(j, basis):
-            removed = proj[j] * proj[k]
-            for g in range(1, groups_prev):
-                removed = removed + proj[g * basis + j] * proj[g * basis + k]
-            gram[j, k] = spread[groups_prev * basis + k, j : j + 1] - jnp.sum(
-                removed, axis=0, keepdims=True
-            )
+        return value
+
+    def gram_of(j, k):
+        removed = proj[j] * proj[k]
+        for g in range(1, groups_prev):
+            removed = removed + proj[g * basis + j] * proj[g * basis + k]
+        return spread[groups_prev * basis + k, j : j + 1] - jnp.sum(
+            removed, axis=0, keepdims=True
+        )
+
+    for k in range(newest):
+        basis_ref[k] = clean(k)
+    gram = {(j, k): gram_of(j, k) for j in range(newest) for k in range(j, newest)}
     lower, inverse = {}, []
-    for j in range(basis):
+    for j in range(newest):
         root = jnp.sqrt(gram[j, j])
         inverse.append(1.0 / root)
         lower[j, j] = root
-        for k in range(j + 1, basis):
+        for k in range(j + 1, newest):
             lower[k, j] = gram[j, k] * inverse[j]
-        for k in range(j + 1, basis):
-            for m in range(k, basis):
+        for k in range(j + 1, newest):
+            for m in range(k, newest):
                 gram[k, m] = gram[k, m] - lower[k, j] * lower[m, j]
+
+    for r in range(rows):
+        done = []
+        for k in range(newest):
+            value = basis_ref[k, r]
+            for j in range(k):
+                value = value - lower[k, j] * done[j]
+            value = value * inverse[k]
+            done.append(value)
+            basis_ref[k, r] = value
+
+    collect(late_gathered, all_sem.at[2])
+    collect(late_gathered, all_sem.at[3])
+    last_line = jnp.sum(late_gathered[...], axis=0) * (1.0 / cells)
+    turned = jnp.broadcast_to(last_line, (tile, tile)).T
+    for g in range(groups_prev + 1):
+        column = turned[g * basis : (g + 1) * basis]
+        spread[g * basis + newest] = column
+        proj[g * basis + newest] = column
+    proj_ref[newest : newest + 1, :] = last_line[:, :prev]
+    square = gram_of(newest, newest)
+    for j in range(newest):
+        value = gram_of(j, newest)
+        for i in range(j):
+            value = value - lower[j, i] * lower[newest, i]
+        lower[newest, j] = value * inverse[j]
+        square = square - lower[newest, j] * lower[newest, j]
+    lower[newest, newest] = jnp.sqrt(square)
+    value = clean(newest)
+    for j in range(newest):
+        value = value - lower[newest, j][None] * basis_ref[j]
+    basis_ref[newest] = value * (1.0 / lower[newest, newest])[None]
 
     row_index = lax.broadcasted_iota(jnp.int32, (basis, tile), 0)
     upper = jnp.zeros((basis, tile), jnp.float32)
@@ -338,27 +525,6 @@
             line = jnp.where(lane[0:1] == k, lower[k, j], line)
         upper = jnp.where(row_index == j, line, upper)
     upper_ref[...] = upper[:, :basis]
-
-    for r in range(rows):
-        done = []
-        for k in range(basis):
-            value = basis_ref[k, r]
-            for j in range(k):
-                value = value - lower[k, j] * done[j]
-            value = value * inverse[k]
-            done.append(value)
-            basis_ref[k, r] = value
-
-    @pl.loop(0, basis)
-    def _(k):
-        for direction in range(4):
-            @pl.when(has[direction])
-            def _(direction=direction):
-                hop(k, direction).wait_send()
-
-    @pl.loop(1, peers)
-    def _(d):
-        deliver(d).wait_send()
 
 
 def store(basis_ref, upper_ref, proj_ref, basis_hbm, upper_hbm, proj_hbm, sem):
@@ -402,21 +568,25 @@
             pltpu.SMEM(start_weights.shape, f32),
             pltpu.VMEM((basis + 1, rows, cols, tile), f32),
             pltpu.VMEM((slots, rows, cols, tile), f32),
+            pltpu.VMEM((basis, rows, cols, tile), f32),
+            pltpu.VMEM((basis, cols, tile), f32),
+            pltpu.VMEM((3, cols, tile // cols, cols, tile), f32),
             pltpu.VMEM((basis, 2, cols, tile), f32),
-            pltpu.VMEM((basis, 2, rows, tile), f32),
-            pltpu.VMEM((basis, 2, rows, tile), f32),
-            pltpu.VMEM((2, cols, tile, tile), f32),
-            pltpu.VMEM((2, rows, tile, tile), f32),
+            pltpu.VMEM((basis, 2, cols, tile), f32),
+            pltpu.VMEM((2, rows, tile), f32),
+            pltpu.VMEM((2, rows, tile), f32),
+            pltpu.VMEM((3, cols, tile, tile), f32),
             pltpu.VMEM((slots - 1, rows, cols, tile), f32),
             pltpu.VMEM((lines, tile), f32),
             pltpu.VMEM((peers, lines, tile), f32),
+            pltpu.VMEM((1, tile), f32),
+            pltpu.VMEM((peers, 1, tile), f32),
             pltpu.VMEM(((prev // basis + 1) * basis, basis, tile), f32),
             pltpu.SemaphoreType.DMA((rows, cols)),
             pltpu.SemaphoreType.DMA((5,)),
             pltpu.SemaphoreType.DMA((basis, 4)),
             pltpu.SemaphoreType.DMA((basis, 4)),
-            pltpu.SemaphoreType.DMA((peers,)),
-            pltpu.SemaphoreType.DMA((peers,)),
+            pltpu.SemaphoreType.DMA((4,)),
         ],
         compiler_params=pltpu.CompilerParams(
             collective_id=0, has_side_effects=True, vmem_limit_bytes=48 * 1024 * 1024

time: 38.4 us -> 36.1 us (0.940)
  Pallas kernels: 37.6 us -> 35.3 us
    pallas_call x1, Pallas kernels: 36.9 us -> 34.6 us  [shards(): pl.pallas_call(functools.partial(kernel, n_rows, n_cols, pitch), out_shap...]
where the time goes in v3:
time: 36.1 us; the launch traced here: 36 us
  Pallas kernels  35.3 us (98%)
  between operations  0.64 us (2%)
    pallas_call x1, Pallas kernels, shards(): pl.pallas_call(functools.partial(kernel, n_rows, n_cols, pitch), out_shap...  34.6 us

profile of v3, /device:TPU:0, one launch (start us, length us, event | category | flops | bytes accessed | tf_op | source)
XLA Modules:
  0.0 36.0 jit_solution(12940803705312435224)
XLA Ops:
  0.6 34.6 %sstep.1 = (f32[8,4,8,128]{3,2,1,0:T(8,128)S(1)}, f32[8,8]{1,0:T(8,128)S(1)}, f32[8,16]{1,0:T(8,128)S(1)}) custom-call(f32[4,8,4,128,128]{4,3,2,1,0:T(8,128)} %blocks_hbm.1, s32[3,4,8]{2,1,0:T(4,128)} %bitcast.2, f32[8]{0:T(128)} %shifts_hbm.1, s32[8]{0:T(128)} %order_hbm.1, f32[16,4,8,128]{3,2,1,0:T(8,128)} %earlier_hbm.1, f32[16]{0:T(128)} %weights_hbm.1), custom_call_target="tpu_custom_call" | custom-call | tf_op jit(solution)/shard_map/sstep/pallas_call | solution.py:553
  35.3 0.7 %store.1 = (f32[8,4,8,128]{3,2,1,0:T(8,128)}, f32[8,8]{1,0:T(8,128)}, f32[8,16]{1,0:T(8,128)}) custom-call(f32[8,4,8,128]{3,2,1,0:T(8,128)S(1)} %get-tuple-element.9.basis_ref, f32[8,8]{1,0:T(8,128)S(1)} %get-tuple-element.10.upper_ref, f32[8,16]{1,0:T(8,128)S(1)} %get-tuple-element.11.proj_ref), custom_call_target="tpu_custom_call" | custom-call | tf_op jit(solution)/shard_map/store/pallas_call | solution.py:597

commit v4 on v3

--- a/solution.py
+++ b/solution.py
@@ -33,6 +33,7 @@
     all_rows = [lax.rem(my_row + d, n_rows) for d in range(n_rows)]
     all_cols = [lax.rem(my_col + d, n_cols) for d in range(n_cols)]
     others = [{"rows": r, "cols": c} for r in all_rows for c in all_cols][1:]
+    others = others[n_cols - 1 :] + others[: n_cols - 1]
     for other in others:
         pl.semaphore_signal(barrier, inc=1, device_id=other, device_id_type=MESH)
 
@@ -55,7 +56,7 @@
     ]
     for copy in small:
         copy.start()
-    for r in range(rows):
+    for r in range(0, 1):
         for c in range(cols):
             load(r, c).start()
 
@@ -367,6 +368,9 @@
 
     small[0].wait()
     small[1].wait()
+    for r in range(1, rows):
+        for c in range(cols):
+            load(r, c).start()
     start = weights_ref[0] * earlier[0]
     for p in range(1, prev):
         start = start + weights_ref[p] * earlier[p]

time: 36.1 us -> 35.4 us (0.981)
  Pallas kernels: 35.3 us -> 34.6 us
    pallas_call x1, Pallas kernels: 34.6 us -> 33.9 us  [shards(): pl.pallas_call(functools.partial(kernel, n_rows, n_cols, pitch), out_shap...]
where the time goes in v4:
time: 35.4 us; the launch traced here: 35.2 us
  Pallas kernels  34.6 us (98%)
  between operations  0.64 us (2%)
    pallas_call x1, Pallas kernels, shards(): pl.pallas_call(functools.partial(kernel, n_rows, n_cols, pitch), out_shap...  33.9 us

profile of v4, /device:TPU:0, one launch (start us, length us, event | category | flops | bytes accessed | tf_op | source)
XLA Modules:
  0.0 35.2 jit_solution(11899872064856642962)
XLA Ops:
  0.6 33.9 %sstep.1 = (f32[8,4,8,128]{3,2,1,0:T(8,128)S(1)}, f32[8,8]{1,0:T(8,128)S(1)}, f32[8,16]{1,0:T(8,128)S(1)}) custom-call(f32[4,8,4,128,128]{4,3,2,1,0:T(8,128)} %blocks_hbm.1, s32[3,4,8]{2,1,0:T(4,128)} %bitcast.2, f32[8]{0:T(128)} %shifts_hbm.1, s32[8]{0:T(128)} %order_hbm.1, f32[16,4,8,128]{3,2,1,0:T(8,128)} %earlier_hbm.1, f32[16]{0:T(128)} %weights_hbm.1), custom_call_target="tpu_custom_call" | custom-call | tf_op jit(solution)/shard_map/sstep/pallas_call | solution.py:557
  34.5 0.7 %store.1 = (f32[8,4,8,128]{3,2,1,0:T(8,128)}, f32[8,8]{1,0:T(8,128)}, f32[8,16]{1,0:T(8,128)}) custom-call(f32[8,4,8,128]{3,2,1,0:T(8,128)S(1)} %get-tuple-element.9.basis_ref, f32[8,8]{1,0:T(8,128)S(1)} %get-tuple-element.10.upper_ref, f32[8,16]{1,0:T(8,128)S(1)} %get-tuple-element.11.proj_ref), custom_call_target="tpu_custom_call" | custom-call | tf_op jit(solution)/shard_map/store/pallas_call | solution.py:601

commit v5 on v4

--- a/solution.py
+++ b/solution.py
@@ -29,14 +29,6 @@
     my_row, my_col = lax.axis_index("rows"), lax.axis_index("cols")
     me = my_row * n_cols + my_col
 
-    barrier = pltpu.get_barrier_semaphore()
-    all_rows = [lax.rem(my_row + d, n_rows) for d in range(n_rows)]
-    all_cols = [lax.rem(my_col + d, n_cols) for d in range(n_cols)]
-    others = [{"rows": r, "cols": c} for r in all_rows for c in all_cols][1:]
-    others = others[n_cols - 1 :] + others[: n_cols - 1]
-    for other in others:
-        pl.semaphore_signal(barrier, inc=1, device_id=other, device_id_type=MESH)
-
     def load(r, c):
         return pltpu.make_async_copy(
             blocks_hbm.at[r, c], blocks.at[r, c], load_sem.at[r, c]
@@ -56,9 +48,18 @@
     ]
     for copy in small:
         copy.start()
-    for r in range(0, 1):
-        for c in range(cols):
-            load(r, c).start()
+
+    barrier = pltpu.get_barrier_semaphore()
+    all_rows = [lax.rem(my_row + d, n_rows) for d in range(n_rows)]
+    all_cols = [lax.rem(my_col + d, n_cols) for d in range(n_cols)]
+    others = [{"rows": r, "cols": c} for r in all_rows for c in all_cols][1:]
+    others = others[n_cols - 1 :] + others[: n_cols - 1]
+    for other in others:
+        pl.semaphore_signal(barrier, inc=1, device_id=other, device_id_type=MESH)
+
+    line_order = [0, rows - 1, *range(1, rows - 1)]
+    for c in range(cols):
+        load(line_order[0], c).start()
 
     for k in range(1, basis + 1):
         fields[k] = jnp.zeros((rows, cols, tile), jnp.float32)
@@ -166,21 +167,33 @@
                     jnp.where(code < 2.5, left, right),
                 )
 
-    def inside(k, first):
+    def line_inside(k, r, shift):
+        for c in range(cols):
+            total = blocks[r, c, 0] * chosen[0, r, c : c + 1]
+            for s in range(1, slots):
+                total = total + blocks[r, c, s] * chosen[s, r, c : c + 1]
+            product = jnp.sum(total.T, axis=0, keepdims=True)
+            fields[k + 1, r, c : c + 1] = product - shift * chosen[0, r, c : c + 1]
+
+    def inside(k):
         shift = shifts_ref[order_ref[k]]
         choose(k)
 
         @pl.loop(0, rows)
         def _(r):
-            if first:
-                for c in range(cols):
-                    load(r, c).wait()
+            line_inside(k, r, shift)
+
+    def inside_first():
+        shift = shifts_ref[order_ref[0]]
+        choose(0)
+        for r in line_order:
             for c in range(cols):
-                total = blocks[r, c, 0] * chosen[0, r, c : c + 1]
-                for s in range(1, slots):
-                    total = total + blocks[r, c, s] * chosen[s, r, c : c + 1]
-                product = jnp.sum(total.T, axis=0, keepdims=True)
-                fields[k + 1, r, c : c + 1] = product - shift * chosen[0, r, c : c + 1]
+                load(r, c).wait()
+            line_inside(0, r, shift)
+            for side in range(2):
+                if r == side * (rows - 1):
+                    gather_line(side)
+                rim_tiles[2, side * rows + r] = pick(r, side * (cols - 1), side + LEFT)
 
     def pick(r, c, direction):
         total = jnp.zeros((tile, tile), jnp.float32)
@@ -189,21 +202,16 @@
             total = jnp.where(code == float(direction), blocks[r, c, s + 1], total)
         return total
 
-    def gather_rim():
-        for side in range(2):
-            @pl.loop(0, cols)
-            def _(c, side=side):
-                total = jnp.zeros((tile, tile), jnp.float32)
-                for s in range(slots - 1):
-                    code = code_table[s, side * (rows - 1), pl.ds(c, 1)]
-                    total = jnp.where(
-                        code == float(side), blocks[side * (rows - 1), c, s + 1], total
-                    )
-                rim_tiles[side, c] = total
-
-            @pl.loop(0, rows)
-            def _(r, side=side):
-                rim_tiles[2, side * rows + r] = pick(r, side * (cols - 1), side + LEFT)
+    def gather_line(side):
+        @pl.loop(0, cols)
+        def _(c):
+            total = jnp.zeros((tile, tile), jnp.float32)
+            for s in range(slots - 1):
+                code = code_table[s, side * (rows - 1), pl.ds(c, 1)]
+                total = jnp.where(
+                    code == float(side), blocks[side * (rows - 1), c, s + 1], total
+                )
+            rim_tiles[side, c] = total
 
     def rim():
         for r in range(rows):
@@ -368,7 +376,7 @@
 
     small[0].wait()
     small[1].wait()
-    for r in range(1, rows):
+    for r in line_order[1:]:
         for c in range(cols):
             load(r, c).start()
     start = weights_ref[0] * earlier[0]
@@ -385,8 +393,7 @@
     for s, lines in enumerate(code_columns()):
         for r, line in enumerate(lines):
             code_table[s, r] = line
-    inside(0, True)
-    gather_rim()
+    inside_first()
 
     receive(0, range(4), True)
     rim()
@@ -396,18 +403,14 @@
     send(1, (ABOVE, BELOW))
     cross[1] = crossing(lines, nothing)
     send(1, (LEFT, RIGHT))
-    inside(1, False)
+    inside(1)
     pack_rim()
 
-    @pl.loop(1, basis - 1)
-    def _(k):
+    for k in range(1, basis - 1):
         finish(k, False)
-        inside(k + 1, False)
-
-        @pl.when(k == 1)
-        def _():
+        inside(k + 1)
+        if k == 1:
             inner(0)
-
         inner(k)
 
     def deliver(src, dst, send_sem, recv_sem):

time: 35.4 us -> 35.3 us (level)
  no operation moved by 1% of the time
where the time goes in v5:
time: 35.3 us; the launch traced here: 35.1 us
  Pallas kernels  34.5 us (98%)
  between operations  0.64 us (2%)
    pallas_call x1, Pallas kernels, shards(): pl.pallas_call(functools.partial(kernel, n_rows, n_cols, pitch), out_shap...  33.8 us

profile of v5, /device:TPU:0, one launch (start us, length us, event | category | flops | bytes accessed | tf_op | source)
XLA Modules:
  0.0 35.1 jit_solution(3917438698047732960)
XLA Ops:
  0.6 33.8 %sstep.1 = (f32[8,4,8,128]{3,2,1,0:T(8,128)S(1)}, f32[8,8]{1,0:T(8,128)S(1)}, f32[8,16]{1,0:T(8,128)S(1)}) custom-call(f32[4,8,4,128,128]{4,3,2,1,0:T(8,128)} %blocks_hbm.1, s32[3,4,8]{2,1,0:T(4,128)} %bitcast.2, f32[8]{0:T(128)} %shifts_hbm.1, s32[8]{0:T(128)} %order_hbm.1, f32[16,4,8,128]{3,2,1,0:T(8,128)} %earlier_hbm.1, f32[16]{0:T(128)} %weights_hbm.1), custom_call_target="tpu_custom_call" | custom-call | tf_op jit(solution)/shard_map/sstep/pallas_call | solution.py:560
  34.4 0.7 %store.1 = (f32[8,4,8,128]{3,2,1,0:T(8,128)}, f32[8,8]{1,0:T(8,128)}, f32[8,16]{1,0:T(8,128)}) custom-call(f32[8,4,8,128]{3,2,1,0:T(8,128)S(1)} %get-tuple-element.9.basis_ref, f32[8,8]{1,0:T(8,128)S(1)} %get-tuple-element.10.upper_ref, f32[8,16]{1,0:T(8,128)S(1)} %get-tuple-element.11.proj_ref), custom_call_target="tpu_custom_call" | custom-call | tf_op jit(solution)/shard_map/store/pallas_call | solution.py:604
